TPU v7x, 32 devices: a whole 2x2x4 slice. The times are simulated.
32 devices in a mesh: region: 4 (over z), depth: 2 (over y), member: 4 (over x, core).
Axes of the slice: x: 2, y: 2, z: 4, core: 2. Of those that a mesh axis runs over, the one named last changes fastest.
Arguments:
- ensemble: bfloat16 [14, 384, 4096], P('depth', 'member', 'region'), may hold values from -6 to 6
- obs_weights: float32 [14], P('depth'), may hold values from -1.5 to 1.5
- obs_tiles: int32 [2048], P('region'), may hold values from 0 to 1023
- obs_values: float32 [2048], P('region'), may hold values from -8 to 8
- obs_error: float32 [2048], P('region'), may hold values from 0.2 to 2
- obs_noise: float32 [384, 2048], P('member', 'region'), may hold values from -6 to 6
Outputs:
- analysis: bfloat16 [14, 384, 4096], P('depth', 'member', 'region')
- inflation: float32 [], replicated
Inputs may be any that keep to these rules, and one draw needn't show every extreme that they name: `obs_tiles`: the tile of the observation, counted within the 1024 tiles of the region whose block holds the observation.
All inputs are finite; a program needn't handle non-finite values.
Results may differ from a plain program's by a relative error of at most 0.011.
Values may be sent and summed in bfloat16 or wider, within the bound.
A program may use at most 64 MiB of HBM per device.

v0:
```python
import jax
import jax.numpy as jnp
from jax import lax
from jax.sharding import PartitionSpec as P

MEMBERS = 384
RADIUS = 1024


def extended(array, sides, width):
    for axis, dim in sides:
        peers, length = (lax.axis_size(axis), array.shape[dim])
        up = [(i, (i + 1) % peers) for i in range(peers - 1)]
        down = [(j, i) for i, j in up]
        last = lax.slice_in_dim(array, length - width, length, axis=dim)
        leading = lax.slice_in_dim(array, 0, width, axis=dim)
        before = lax.ppermute(last, axis, up)
        after = lax.ppermute(leading, axis, down)
        array = jnp.concatenate([before, array, after], axis=dim)
    return array


def regress(
    anomalies, own_anom, state_mean, obs_anom, perturbed, factor, obs_pos, first_tile, infl_root
):
    var_count = anomalies.shape[0]
    tile_count = anomalies.shape[2]
    block = 128

    def one_block(block_index, output):
        block_start = block_index * block
        slab = lax.dynamic_slice_in_dim(anomalies, block_start, block, 2)
        own_slab = lax.dynamic_slice_in_dim(own_anom, block_start, block, 2)
        means = lax.dynamic_slice_in_dim(state_mean, block_start, block, 1)
        covariance = jnp.einsum(
            "lmt,mj->ltj", slab, obs_anom, preferred_element_type=jnp.float32
        ) / (MEMBERS - 1)
        tile_pos = (first_tile + block_start + jnp.arange(block, dtype=jnp.int32)).astype(
            jnp.float32
        )
        closeness = jnp.maximum(0.0, 1.0 - jnp.abs(tile_pos[:, None] - obs_pos[None, :]) / RADIUS)
        kalman_gain = (covariance * (closeness * closeness * factor[None, :])[None]).astype(
            jnp.bfloat16
        )
        increment = jnp.einsum(
            "ltj,mj->lmt", kalman_gain, perturbed, preferred_element_type=jnp.float32
        )
        updated = (means[:, None, :] + infl_root * own_slab.astype(jnp.float32) + increment).astype(
            jnp.bfloat16
        )
        return lax.dynamic_update_slice_in_dim(output, updated, block_start, 2)

    output = jnp.zeros((var_count, perturbed.shape[0], tile_count), jnp.bfloat16)
    return lax.fori_loop(0, tile_count // block, one_block, output)


def shards(ensemble, obs_weights, obs_tiles, obs_values, obs_error, obs_noise):
    tile_count = ensemble.shape[2]
    own_members = ensemble.shape[1]
    obs_count = obs_tiles.shape[0]
    member_sum = jnp.sum(ensemble, axis=1, dtype=jnp.float32)
    picked = jnp.take(ensemble, obs_tiles, axis=2).astype(jnp.float32)
    partial_pred = jnp.einsum("lmk,l->mk", picked, obs_weights, precision=lax.Precision.HIGHEST)
    predicted = lax.psum(partial_pred, "depth")
    totals = lax.psum(
        (member_sum, jnp.sum(predicted, axis=0), jnp.sum(predicted * predicted, axis=0)), "member"
    )
    state_mean = totals[0] / MEMBERS
    obs_mean = totals[1] / MEMBERS
    obs_dev = predicted - obs_mean[None, :]
    obs_spread = (totals[2] - MEMBERS * obs_mean * obs_mean) / (MEMBERS - 1)
    innovation = obs_values - obs_mean
    global_sums = lax.psum(
        (jnp.sum(innovation * innovation), jnp.sum(obs_spread + obs_error)), "region"
    )
    inflation = global_sums[0] / global_sums[1]
    infl_root = jnp.sqrt(inflation)
    factor = inflation / (inflation * obs_spread + obs_error)
    obs_anom = obs_dev.astype(jnp.bfloat16)
    perturbed = (
        innovation[None, :] + jnp.sqrt(obs_error)[None, :] * obs_noise - infl_root * obs_dev
    ).astype(jnp.bfloat16)
    first_tile = lax.axis_index("region") * tile_count
    obs_pos = (first_tile + obs_tiles).astype(jnp.float32)
    stacked = jnp.concatenate([obs_anom, perturbed], axis=0)
    widened = extended(stacked, (("region", 1),), obs_count)
    near_anom = widened[:own_members]
    near_pert = widened[own_members:]
    scalars = jnp.stack([factor, obs_pos], axis=0)
    wide_scalars = extended(scalars, (("region", 1),), obs_count)
    near_factor = wide_scalars[0]
    near_pos = wide_scalars[1]
    anomalies = (ensemble.astype(jnp.float32) - state_mean[:, None, :]).astype(jnp.bfloat16)
    all_anom, all_obs_anom = (
        lax.all_gather(anomalies, "member", axis=1, tiled=True),
        lax.all_gather(near_anom, "member", axis=0, tiled=True),
    )
    analysis = regress(
        all_anom,
        anomalies,
        state_mean,
        all_obs_anom,
        near_pert,
        near_factor,
        near_pos,
        first_tile,
        infl_root,
    )
    return (analysis, inflation)


def solution(mesh):
    return jax.shard_map(
        shards,
        mesh=mesh,
        in_specs=(
            P("depth", "member", "region"),
            P("depth"),
            P("region"),
            P("region"),
            P("region"),
            P("member", "region"),
        ),
        out_specs=(P("depth", "member", "region"), P()),
        check_vma=False,
    )
```

profile of v0, /device:TPU:0, one launch (start us, length us, event | category | flops | bytes accessed | tf_op | source)
XLA Modules:
  0.0 185.1 jit_solution(7628334277064460269)
XLA Ops:
  8.6 3.2 %copy.8 = bf16[7,96,1024]{1,0,2:T(8,128)(2,1)S(1)} copy(bf16[7,96,1024]{2,1,0:T(8,128)(2,1)} %param.8) | data formatting | bytes 2752512 | tf_op args[0]
  11.8 1.8 gather_fusion
  13.7 1.8 select_bitcast_fusion
  15.4 1.0 copy.9
  16.5 0.8 fusion.20
  17.3 0.7 copy.12
  18.4 25.0 %all-reduce.4.cloned.1.call-done = f32[96,512]{1,0:T(8,128)} async-done(((f32[96,512]{1,0:T(8,128)}), f32[96,512]{1,0:T(8,128)}) %all-reduce.4.cloned.1.call-update) | async-done | bytes 196624 | tf_op jit(solution)/shard_map/psum | solution.py:64
  43.3 1.0 multiply_reduce_fusion
  44.3 10.8 %all-reduce = (f32[7,1024]{1,0:T(8,128)S(1)}, f32[512]{0:T(512)S(1)}, f32[512]{0:T(512)S(1)}) all-reduce(f32[7,1024]{1,0:T(8,128)S(1)} %convert_reduce_fusion, f32[512]{0:T(512)S(1)} %get-tuple-element.188, f32[512]{0:T(512)S(1)} %get-tuple-element.187), channel_id=1, replica_groups=mesh['region'=4,'depth'=2,'member'=4] {'member'}, use_global_device_ids=true, to_apply=%region_1.2 | all-reduce | flops 8192 | bytes 65536 | tf_op jit(solution)/shard_map/psum | solution.py:65
  55.7 12.3 %all-reduce.1 = (f32[]{:T(128)}, f32[]{:T(128)}) all-reduce(f32[]{:T(128)} %get-tuple-element.216, f32[]{:T(128)} %get-tuple-element.229), channel_id=1, replica_groups=mesh['region'=4,'depth'=2,'member'=4] {'region'}, use_global_device_ids=true, to_apply=%region_6.7 | all-reduce | flops 2 | bytes 16 | tf_op jit(solution)/shard_map/psum | solution.py:73
  69.5 1.0 subtract_convert_fusion.1
  70.5 1.3 collective-permute-start.1
  71.8 4.6 %collective-permute-start = (bf16[192,512]{1,0:T(8,128)(2,1)S(1)}, bf16[192,512]{1,0:T(8,128)(2,1)S(1)}, u32[]{:S(2)}, u32[]{:S(2)}) collective-permute-start(bf16[192,512]{1,0:T(8,128)(2,1)S(1)} %pad_maximum_fusion.1), channel_id=1, source_target_pairs={{0,8},{8,16},{16,24},{1,9},{9,17},{17,25},{2,10},{10,18},{18,26},{... | collective-permute-start | bytes 589832 | tf_op jit(solution)/shard_map/ppermute | solution.py:17
  76.4 1.7 collective-permute-done.1
  78.1 1.5 collective-permute-done
  79.6 0.8 fusion.23
  80.4 1.4 fusion.18
  81.9 1.3 collective-permute-start.3
  83.2 5.0 %collective-permute-start.2 = (f32[2,512]{1,0:T(2,128)S(1)}, f32[2,512]{1,0:T(2,128)S(1)}, u32[]{:S(2)}, u32[]{:S(2)}) collective-permute-start(f32[2,512]{1,0:T(2,128)S(1)} %pad_maximum_fusion.3), channel_id=1, source_target_pairs={{0,8},{8,16},{16,24},{1,9},{9,17},{17,25},{2,10},{10,18},{18,26},{... | collective-permute-start | bytes 12296 | tf_op jit(solution)/shard_map/ppermute | solution.py:17
  88.2 1.3 collective-permute-done.2
  89.6 7.4 %all-gather.5.cloned.1.call-done = bf16[384,1536]{1,0:T(8,128)(2,1)} async-done(((bf16[96,1536]{1,0:T(8,128)(2,1)}), bf16[384,1536]{1,0:T(8,128)(2,1)}) %all-gather.5.cloned.1.call-update) | async-done | bytes 1179664 | tf_op jit(solution)/shard_map/all_gather | solution.py:96
  97.0 44.1 %all-gather.3.cloned.1.call-done = bf16[7,384,1024]{2,1,0:T(8,128)(2,1)} async-done(((bf16[7,96,1024]{2,1,0:T(8,128)(2,1)}), bf16[7,384,1024]{2,1,0:T(8,128)(2,1)}) %all-gather.3.cloned.1.call-update) | async-done | bytes 5505040 | tf_op jit(solution)/shard_map/all_gather | solution.py:95
  141.2 35.1 %while.13 = (s32[]{:T(128)}, bf16[7,96,1024]{2,1,0:T(8,128)(2,1)S(1)}, f32[7,1024]{1,0:T(8,128)S(1)}, f32[]{:T(128)}, bf16[7,96,1024]{2,1,0:T(8,128)(2,1)}, /*in...) while((s32[]{:T(128)}, ...), condition=%wide.region_12.13_spmd, body=%wide.region_11.12_spmd.sunk | while | flops 1325961472 | bytes 4130527 | solution.py:54
  141.6 4.0 %fusion.33 = bf16[7,96,1024]{2,1,0:T(8,128)(2,1)S(1)} fusion(bf16[7,96,1024]{2,1,0:T(8,128)(2,1)S(1)} %get-tuple-element.314, s32[]{:T(128)S(6)} %select_n.27, f32[128,1536]{1,0:T(8,128)S(1)} %multiply_multiply_fusion.2, bf16[384,1536]{1,0:T(8,128)(2,1)} %get-tuple-element.335, bf16[7,384,1024]{2,1,0:T(8,128)(2,1)} %get-tuple-element.334, ...), kind=kOutput, calls=%fused_computation.7.clone.1 | convolution fusion | flops 1324388352 | bytes 3298816 | tf_op jit(solution)/shard_map/while/body/eval_jaxpr/ltj,mj->lmt/dot_general | solution.py:45
  146.0 4.0 %fusion.33 = bf16[7,96,1024]{2,1,0:T(8,128)(2,1)S(1)} fusion(bf16[7,96,1024]{2,1,0:T(8,128)(2,1)S(1)} %get-tuple-element.314, s32[]{:T(128)S(6)} %select_n.27, f32[128,1536]{1,0:T(8,128)S(1)} %multiply_multiply_fusion.2, bf16[384,1536]{1,0:T(8,128)(2,1)} %get-tuple-element.335, bf16[7,384,1024]{2,1,0:T(8,128)(2,1)} %get-tuple-element.334, ...), kind=kOutput, calls=%fused_computation.7.clone.1 | convolution fusion | flops 1324388352 | bytes 3298816 | tf_op jit(solution)/shard_map/while/body/eval_jaxpr/ltj,mj->lmt/dot_general | solution.py:45
  150.4 4.0 %fusion.33 = bf16[7,96,1024]{2,1,0:T(8,128)(2,1)S(1)} fusion(bf16[7,96,1024]{2,1,0:T(8,128)(2,1)S(1)} %get-tuple-element.314, s32[]{:T(128)S(6)} %select_n.27, f32[128,1536]{1,0:T(8,128)S(1)} %multiply_multiply_fusion.2, bf16[384,1536]{1,0:T(8,128)(2,1)} %get-tuple-element.335, bf16[7,384,1024]{2,1,0:T(8,128)(2,1)} %get-tuple-element.334, ...), kind=kOutput, calls=%fused_computation.7.clone.1 | convolution fusion | flops 1324388352 | bytes 3298816 | tf_op jit(solution)/shard_map/while/body/eval_jaxpr/ltj,mj->lmt/dot_general | solution.py:45
  154.8 4.0 %fusion.33 = bf16[7,96,1024]{2,1,0:T(8,128)(2,1)S(1)} fusion(bf16[7,96,1024]{2,1,0:T(8,128)(2,1)S(1)} %get-tuple-element.314, s32[]{:T(128)S(6)} %select_n.27, f32[128,1536]{1,0:T(8,128)S(1)} %multiply_multiply_fusion.2, bf16[384,1536]{1,0:T(8,128)(2,1)} %get-tuple-element.335, bf16[7,384,1024]{2,1,0:T(8,128)(2,1)} %get-tuple-element.334, ...), kind=kOutput, calls=%fused_computation.7.clone.1 | convolution fusion | flops 1324388352 | bytes 3298816 | tf_op jit(solution)/shard_map/while/body/eval_jaxpr/ltj,mj->lmt/dot_general | solution.py:45
  159.2 4.0 %fusion.33 = bf16[7,96,1024]{2,1,0:T(8,128)(2,1)S(1)} fusion(bf16[7,96,1024]{2,1,0:T(8,128)(2,1)S(1)} %get-tuple-element.314, s32[]{:T(128)S(6)} %select_n.27, f32[128,1536]{1,0:T(8,128)S(1)} %multiply_multiply_fusion.2, bf16[384,1536]{1,0:T(8,128)(2,1)} %get-tuple-element.335, bf16[7,384,1024]{2,1,0:T(8,128)(2,1)} %get-tuple-element.334, ...), kind=kOutput, calls=%fused_computation.7.clone.1 | convolution fusion | flops 1324388352 | bytes 3298816 | tf_op jit(solution)/shard_map/while/body/eval_jaxpr/ltj,mj->lmt/dot_general | solution.py:45
  163.6 4.0 %fusion.33 = bf16[7,96,1024]{2,1,0:T(8,128)(2,1)S(1)} fusion(bf16[7,96,1024]{2,1,0:T(8,128)(2,1)S(1)} %get-tuple-element.314, s32[]{:T(128)S(6)} %select_n.27, f32[128,1536]{1,0:T(8,128)S(1)} %multiply_multiply_fusion.2, bf16[384,1536]{1,0:T(8,128)(2,1)} %get-tuple-element.335, bf16[7,384,1024]{2,1,0:T(8,128)(2,1)} %get-tuple-element.334, ...), kind=kOutput, calls=%fused_computation.7.clone.1 | convolution fusion | flops 1324388352 | bytes 3298816 | tf_op jit(solution)/shard_map/while/body/eval_jaxpr/ltj,mj->lmt/dot_general | solution.py:45
  167.9 4.0 %fusion.33 = bf16[7,96,1024]{2,1,0:T(8,128)(2,1)S(1)} fusion(bf16[7,96,1024]{2,1,0:T(8,128)(2,1)S(1)} %get-tuple-element.314, s32[]{:T(128)S(6)} %select_n.27, f32[128,1536]{1,0:T(8,128)S(1)} %multiply_multiply_fusion.2, bf16[384,1536]{1,0:T(8,128)(2,1)} %get-tuple-element.335, bf16[7,384,1024]{2,1,0:T(8,128)(2,1)} %get-tuple-element.334, ...), kind=kOutput, calls=%fused_computation.7.clone.1 | convolution fusion | flops 1324388352 | bytes 3298816 | tf_op jit(solution)/shard_map/while/body/eval_jaxpr/ltj,mj->lmt/dot_general | solution.py:45
  172.3 4.0 %fusion.33 = bf16[7,96,1024]{2,1,0:T(8,128)(2,1)S(1)} fusion(bf16[7,96,1024]{2,1,0:T(8,128)(2,1)S(1)} %get-tuple-element.314, s32[]{:T(128)S(6)} %select_n.27, f32[128,1536]{1,0:T(8,128)S(1)} %multiply_multiply_fusion.2, bf16[384,1536]{1,0:T(8,128)(2,1)} %get-tuple-element.335, bf16[7,384,1024]{2,1,0:T(8,128)(2,1)} %get-tuple-element.334, ...), kind=kOutput, calls=%fused_computation.7.clone.1 | convolution fusion | flops 1324388352 | bytes 3298816 | tf_op jit(solution)/shard_map/while/body/eval_jaxpr/ltj,mj->lmt/dot_general | solution.py:45
  176.4 1.1 copy-done.2
  (71 shorter events, 5.4 us)
Async XLA Ops:
  7.2 9.3 %copy-start = (f32[7]{0:T(128)S(1)}, f32[7]{0:T(128)}, u32[]{:S(2)}) copy-start(f32[7]{0:T(128)} %param.9) | copy-start | bytes 88
  7.2 36.1 %all-reduce.4.cloned.1.call-start = ((), (), s32[]{:S(2)}) async-start(), calls=%async_computation | async-start | bytes 393216 | tf_op jit(solution)/shard_map/psum | solution.py:64
  15.4 2.6 %copy-start.1 = (bf16[7,96,1024]{2,1,0:T(8,128)(2,1)S(1)}, bf16[7,96,1024]{2,1,0:T(8,128)(2,1)}, u32[]{:S(2)}) copy-start(bf16[7,96,1024]{2,1,0:T(8,128)(2,1)} %param.8) | copy-start | bytes 4128772
  16.5 38.6 %copy-start.4 = (f32[512]{0:T(512)S(1)}, f32[512]{0:T(512)}, u32[]{:S(2)}) copy-start(f32[512]{0:T(512)} %param.12) | copy-start | bytes 6148
  16.5 38.6 %copy-start.5 = (f32[512]{0:T(512)S(1)}, f32[512]{0:T(512)}, u32[]{:S(2)}) copy-start(f32[512]{0:T(512)} %param.11) | copy-start | bytes 6148
  17.3 52.2 %copy-start.3 = (f32[96,512]{1,0:T(8,128)S(1)}, f32[96,512]{1,0:T(8,128)}, u32[]{:S(2)}) copy-start(f32[96,512]{1,0:T(8,128)} %param.13) | copy-start | bytes 589828
  18.0 79.0 %all-gather.5.cloned.1.call-start = ((), (), s32[]{:S(2)}) async-start(), calls=%async_computation.2 | async-start | bytes 1474560 | tf_op jit(solution)/shard_map/all_gather | solution.py:96
  70.5 7.6 %collective-permute-start.1 = (bf16[192,512]{1,0:T(8,128)(2,1)S(1)}, bf16[192,512]{1,0:T(8,128)(2,1)S(1)}, u32[]{:S(2)}, u32[]{:S(2)}) collective-permute-start(bf16[192,512]{1,0:T(8,128)(2,1)S(1)} %pad_maximum_fusion.1), channel_id=1, source_target_pairs={{8,0},{16,8},{24,16},{9,1},{17,9},{25,17},{10,2},{18,10},{26,18},{... | collective-permute-start | bytes 589832 | tf_op jit(solution)/shard_map/ppermute | solution.py:18
  71.8 7.7 %collective-permute-start = (bf16[192,512]{1,0:T(8,128)(2,1)S(1)}, bf16[192,512]{1,0:T(8,128)(2,1)S(1)}, u32[]{:S(2)}, u32[]{:S(2)}) collective-permute-start(bf16[192,512]{1,0:T(8,128)(2,1)S(1)} %pad_maximum_fusion.1), channel_id=1, source_target_pairs={{0,8},{8,16},{16,24},{1,9},{9,17},{17,25},{2,10},{10,18},{18,26},{... | collective-permute-start | bytes 589832 | tf_op jit(solution)/shard_map/ppermute | solution.py:17
  80.4 60.7 %all-gather.3.cloned.1.call-start = ((), (), s32[]{:S(2)}) async-start(), calls=%async_computation.1 | async-start | bytes 6881280 | tf_op jit(solution)/shard_map/all_gather | solution.py:95
  81.9 6.3 %collective-permute-start.3 = (f32[2,512]{1,0:T(2,128)S(1)}, f32[2,512]{1,0:T(2,128)S(1)}, u32[]{:S(2)}, u32[]{:S(2)}) collective-permute-start(f32[2,512]{1,0:T(2,128)S(1)} %pad_maximum_fusion.3), channel_id=1, source_target_pairs={{8,0},{16,8},{24,16},{9,1},{17,9},{25,17},{10,2},{18,10},{26,18},{... | collective-permute-start | bytes 12296 | tf_op jit(solution)/shard_map/ppermute | solution.py:18
  83.2 6.3 %collective-permute-start.2 = (f32[2,512]{1,0:T(2,128)S(1)}, f32[2,512]{1,0:T(2,128)S(1)}, u32[]{:S(2)}, u32[]{:S(2)}) collective-permute-start(f32[2,512]{1,0:T(2,128)S(1)} %pad_maximum_fusion.3), channel_id=1, source_target_pairs={{0,8},{8,16},{16,24},{1,9},{9,17},{17,25},{2,10},{10,18},{18,26},{... | collective-permute-start | bytes 12296 | tf_op jit(solution)/shard_map/ppermute | solution.py:17
  176.3 1.1 copy-start.2
Sparse Core Ops, SparseCore 0:
  18.1 25.1 all-reduce.3
  80.5 16.4 all-gather.4
  99.1 41.8 all-gather.2
where the time goes:
time: 186 us; the launch traced here: 185 us
  waiting for transfers between devices  80.9 us (43%)
  matrix products  32.7 us (18%)
  blocking collectives  23.2 us (12%)
  between operations  16.5 us (9%)
  starting transfers between devices  12.3 us (7%)
  other arithmetic  10.1 us (5%)
  local copies, waits for them, and re-layouts  8.89 us (5%)
    all_gather x1, waiting for transfers between devices, shards(): lax.all_gather(anomalies, 'member', axis=1, tiled=True)  44.1 us
    dot_general x8, matrix products, one_block(): jnp.einsum('ltj,mj->lmt', kalman_gain, perturbed, preferred_element_type=...  31.9 us
    psum x1, waiting for transfers between devices, shards(): predicted = lax.psum(partial_pred, 'depth')  25 us
    psum x1, blocking collectives, shards(): lax.psum((jnp.sum(innovation * innovation), jnp.sum(obs_spread + obs_erro...  12.3 us
    psum x1, blocking collectives, shards(): lax.psum((member_sum, jnp.sum(predicted, axis=0), jnp.sum(predicted * pre...  10.8 us
    ppermute x2, starting transfers between devices, extended(): before = lax.ppermute(last, axis, up)  9.57 us
    all_gather x1, waiting for transfers between devices, shards(): lax.all_gather(near_anom, 'member', axis=0, tiled=True)  7.4 us
    unnamed x13, local copies, waits for them, and re-layouts  4.34 us
  transfers between devices with their start and end apart: 7, of which 6 were waited for; matrix products, arithmetic and copies ran while one was open for 1% of the time, Pallas kernels for 0%

commit v1 on v0

v1 whole, which is shorter than its diff:
```python
import functools

import jax
import jax.numpy as jnp
from jax import lax
from jax.experimental import pallas as pl
from jax.experimental.pallas import tpu as pltpu
from jax.sharding import PartitionSpec as P

RADIUS = 1024
F32 = jnp.float32
BF16 = jnp.bfloat16
MESH = pl.DeviceIdType.MESH


def kernel(
    sizes,
    weights,
    ensemble,
    tiles,
    values,
    errors,
    noise,
    out,
    infl_out,
    own,
    gathered,
    noise_v,
    part,
    part_in,
    sums,
    squares,
    totals,
    stats,
    obs,
    pert,
    obs_t,
    taper,
    anom,
    gain,
    result,
    local_sem,
    send_e,
    recv_e,
    send_s,
    recv_s,
    send_p,
    recv_p,
    send_q,
    recv_q,
    send_o,
    recv_o,
    send_g,
    recv_g,
    send_z,
    recv_z,
    send_st,
    recv_st,
    send_ps,
    recv_ps,
    send_pz,
    recv_pz,
    send_out,
    recv_out,
    own_out,
):
    nr, nd, nm, nl, mm, tt, kk = sizes
    ng = nm // 2
    half = tt // 2
    members = nm * mm
    r = lax.axis_index("region")
    d = lax.axis_index("depth")
    me = lax.axis_index("member")
    q = me // 2
    c = me % 2
    sib = 2 * q + (1 - c)
    has_side = (r > 0, r < nr - 1)

    def dev(region=None, depth=None, member=None):
        return {
            "region": r if region is None else region,
            "depth": d if depth is None else depth,
            "member": me if member is None else member,
        }

    def rdma(src, dst, ssem, rsem, device):
        return pltpu.make_async_remote_copy(
            src_ref=src,
            dst_ref=dst,
            send_sem=ssem,
            recv_sem=rsem,
            device_id=device,
            device_id_type=MESH,
        )

    local_own = pltpu.make_async_copy(ensemble, own, local_sem.at[0])
    local_own.start()
    local_half = pltpu.make_async_copy(
        ensemble.at[:, :, pl.ds(pl.multiple_of(c * half, 128), half)],
        gathered.at[:, me],
        local_sem.at[1],
    )
    local_half.start()
    local_noise = pltpu.make_async_copy(noise, noise_v, local_sem.at[2])
    local_noise.start()

    group = [(i, j) for i in range(nd) for j in range(nm) if i or j]
    barrier = pltpu.get_barrier_semaphore()
    signals = 0
    for i, j in group:
        pl.semaphore_signal(
            barrier,
            inc=1,
            device_id=dev(depth=(d + i) % nd, member=(me + j) % nm),
            device_id_type=MESH,
        )
        signals += 1
    for i in range(1, nr):
        pl.semaphore_signal(
            barrier, inc=1, device_id=dev(region=(r + i) % nr), device_id_type=MESH
        )
        signals += 1
    for i in (1, nr - 1):
        pl.semaphore_signal(
            barrier,
            inc=1,
            device_id=dev(region=(r + i) % nr, member=sib),
            device_id_type=MESH,
        )
        signals += 1
    pl.semaphore_wait(barrier, signals)

    def bulk(l, j):
        to = (me + j) % nm
        return rdma(
            ensemble.at[l, :, pl.ds(pl.multiple_of((to % 2) * half, 128), half)],
            gathered.at[l, me],
            send_e.at[l, j],
            recv_e.at[l, me],
            dev(member=to),
        )

    def send_bulk(l):
        for j in range(1, nm):
            bulk(l, j).start()

    send_bulk(0)

    local_own.wait()
    total = own[0].astype(F32) * weights[0]
    for l in range(1, nl):
        total = total + own[l].astype(F32) * weights[l]
    hi = total.astype(BF16)
    rest = total - hi.astype(F32)
    mid = rest.astype(BF16)
    low = (rest - mid.astype(F32)).astype(BF16)
    tile_ids = lax.broadcasted_iota(jnp.int32, (tt, kk), 0)
    onehot = jnp.where(tile_ids == tiles[...], 1.0, 0.0).astype(BF16)
    picked = (
        jnp.dot(hi, onehot, preferred_element_type=F32)
        + jnp.dot(mid, onehot, preferred_element_type=F32)
        + jnp.dot(low, onehot, preferred_element_type=F32)
    )
    part[...] = picked
    here = d * nm + me
    sums[here] = jnp.broadcast_to(jnp.sum(picked, axis=0, keepdims=True), (8, kk))

    def part_copy(i):
        to = (d + i) % nd
        return rdma(part, part_in.at[d], send_p.at[i], recv_p.at[d], dev(depth=to))

    def part_from(i):
        frm = (d + i) % nd
        return rdma(part, part_in.at[frm], send_p.at[i], recv_p.at[frm], dev(depth=frm))

    def sum_copy(i, j):
        return rdma(
            sums.at[here],
            sums.at[here],
            send_s.at[i * nm + j],
            recv_s.at[here],
            dev(depth=(d + i) % nd, member=(me + j) % nm),
        )

    def sum_from(i, j):
        slot = ((d + i) % nd) * nm + (me + j) % nm
        return rdma(
            sums.at[slot],
            sums.at[slot],
            send_s.at[i * nm + j],
            recv_s.at[slot],
            dev(depth=(d + i) % nd, member=(me + j) % nm),
        )

    for i, j in group:
        sum_copy(i, j).start()
    for i in range(1, nd):
        part_copy(i).start()
    send_bulk(1)

    for i, j in group:
        sum_from(i, j).wait_recv()
    mean_sum = sums[0][:1]
    for i in range(1, nd * nm):
        mean_sum = mean_sum + sums[i][:1]
    obs_mean = mean_sum / members
    predicted = part[...]
    for i in range(1, nd):
        part_from(i).wait_recv()
        predicted = predicted + part_in[(d + i) % nd]
    deviation = predicted - obs_mean
    part_in[d] = deviation
    obs[me, :, kk : 2 * kk] = deviation.astype(BF16)
    squares[me] = jnp.broadcast_to(
        jnp.sum(deviation * deviation, axis=0, keepdims=True), (8, kk)
    )

    def square_copy(j, slot):
        return rdma(
            squares.at[slot],
            squares.at[slot],
            send_q.at[j],
            recv_q.at[slot],
            dev(member=(me + j) % nm),
        )

    def obs_copy(j, slot):
        block = obs.at[slot, :, pl.ds(kk, kk)]
        return rdma(block, block, send_o.at[j], recv_o.at[slot], dev(member=(me + j) % nm))

    def side_obs(side, slot, pair, to):
        window = 2 * kk if side == 0 else 0
        return rdma(
            obs.at[slot, :, pl.ds(kk, kk)],
            obs.at[slot, :, pl.ds(window, kk)],
            send_z.at[side, pair, to],
            recv_z.at[1 - side, slot],
            dev(region=r + (2 * side - 1), member=2 * q + to),
        )

    for j in range(1, nm):
        square_copy(j, me).start()
    for j in range(1, nm):
        obs_copy(j, me).start()
    for side in (0, 1):

        @pl.when(has_side[side])
        def _():
            for to in (0, 1):
                side_obs(side, me, 0, to).start()

        @pl.when(jnp.logical_not(has_side[side]))
        def _():
            window = 0 if side == 0 else 2 * kk
            obs[:, :, window : window + kk] = jnp.zeros((nm, mm, kk), BF16)
            pert[:, :, window : window + kk] = jnp.zeros((2, mm, kk), BF16)
            stats[2 * side] = jnp.zeros((8, kk), F32)

    def send_rest(l, carry):
        send_bulk(l)
        return carry

    lax.fori_loop(2, nl, send_rest, 0)

    for j in range(1, nm):
        square_copy(j, (me + j) % nm).wait_recv()
    square_sum = squares[0][:1]
    for j in range(1, nm):
        square_sum = square_sum + squares[j][:1]
    spread = square_sum / (members - 1)
    error = errors[...]
    innovation = values[...] - obs_mean
    first = jnp.sum(innovation * innovation, axis=1, keepdims=True)
    second = jnp.sum(spread + error, axis=1, keepdims=True)
    rows = lax.broadcasted_iota(jnp.int32, (8, 128), 0)
    totals[r] = jnp.where(rows == 0, first, second)

    def total_copy(i, slot):
        return rdma(
            totals.at[slot],
            totals.at[slot],
            send_g.at[i],
            recv_g.at[slot],
            dev(region=(r + i) % nr),
        )

    for i in range(1, nr):
        total_copy(i, r).start()

    for g in range(1, ng):
        slot = 2 * ((q + g) % ng) + c
        obs_copy(2 * g, slot).wait_recv()
        for side in (0, 1):

            @pl.when(has_side[side])
            def _():
                for to in (0, 1):
                    side_obs(side, slot, g, to).start()

    for i in range(1, nr):
        total_copy(i, (r + i) % nr).wait_recv()
    grand = totals[0]
    for i in range(1, nr):
        grand = grand + totals[i]
    inflation = grand[0:1, 0:1] / grand[1:2, 0:1]
    root = jnp.sqrt(inflation)
    infl_out[...] = inflation
    factor = inflation / (inflation * spread + error)
    srow = lax.broadcasted_iota(jnp.int32, (8, kk), 0)
    stats[1] = jnp.where(srow == 0, tiles[...].astype(F32), factor / (members - 1))
    local_noise.wait()
    pert[c, :, kk : 2 * kk] = (
        innovation + jnp.sqrt(error) * noise_v[...] - root * part_in[d]
    ).astype(BF16)

    def stat_copy(side):
        return rdma(
            stats.at[1],
            stats.at[2 - 2 * side],
            send_st.at[side],
            recv_st.at[1 - side],
            dev(region=r + (2 * side - 1)),
        )

    def sib_pert(slot):
        block = pert.at[slot, :, pl.ds(kk, kk)]
        return rdma(block, block, send_ps.at[0], recv_ps.at[0], dev(member=sib))

    def side_pert(side, slot, to):
        window = 2 * kk if side == 0 else 0
        return rdma(
            pert.at[slot, :, pl.ds(kk, kk)],
            pert.at[slot, :, pl.ds(window, kk)],
            send_pz.at[side, to],
            recv_pz.at[1 - side, slot],
            dev(region=r + (2 * side - 1), member=2 * q + to),
        )

    sib_pert(c).start()
    for side in (0, 1):

        @pl.when(has_side[side])
        def _():
            stat_copy(side).start()
            for to in (0, 1):
                side_pert(side, c, to).start()

    for side in (0, 1):

        @pl.when(has_side[side])
        def _():
            rdma(
                stats.at[1], stats.at[2 * side], send_st.at[side], recv_st.at[side], dev(region=r + (2 * side - 1))
            ).wait_recv()

    lane = (lax.broadcasted_iota(jnp.int32, (kk, half), 1) + c * half).astype(F32)
    for w in range(3):
        columns = stats[w].T
        position = columns[:, 0:1] + float((w - 1) * tt)
        close = jnp.maximum(0.0, 1.0 - jnp.abs(lane - position) * (1.0 / RADIUS))
        taper[w * kk : (w + 1) * kk] = close * close * columns[:, 1:2]

    for j in range(1, nm):
        slot = (me + j) % nm
        if j % 2 == 1:
            obs_copy(j, slot).wait_recv()
    for side in (0, 1):

        @pl.when(has_side[side])
        def _():
            for slot in range(nm):
                block = obs.at[slot, :, pl.ds(2 * kk * side, kk)]
                rdma(
                    block, block, send_z.at[side, 0, 0], recv_z.at[side, slot], dev(region=r + (2 * side - 1))
                ).wait_recv()

    for w in range(3):
        for g in range(nm):
            block = obs[g, :, w * kk : (w + 1) * kk].astype(F32)
            obs_t[w * kk : (w + 1) * kk, g * mm : (g + 1) * mm] = block.T.astype(BF16)

    sib_pert(1 - c).wait_recv()
    for side in (0, 1):

        @pl.when(has_side[side])
        def _():
            for slot in (0, 1):
                block = pert.at[slot, :, pl.ds(2 * kk * side, kk)]
                rdma(
                    block, block, send_pz.at[side, 0], recv_pz.at[side, slot], dev(region=r + (2 * side - 1))
                ).wait_recv()

    local_half.wait()
    step = kk // 2

    def out_half(l, which):
        return out.at[l, :, pl.ds(pl.multiple_of(which * half, 128), half)]

    def out_local(l):
        return pltpu.make_async_copy(result.at[l, c], out_half(l, c), own_out.at[l])

    def out_remote(l):
        return rdma(
            result.at[l, 1 - c], out_half(l, c), send_out.at[l], recv_out.at[l], dev(member=sib)
        )

    def out_from(l):
        return rdma(
            result.at[l, 1 - c], out_half(l, 1 - c), send_out.at[l], recv_out.at[l], dev(member=sib)
        )

    def one_variable(l, carry):
        for j in range(1, nm):
            slot = (me + j) % nm
            rdma(
                gathered.at[l, slot],
                gathered.at[l, slot],
                send_e.at[l, j],
                recv_e.at[l, slot],
                dev(member=slot),
            ).wait_recv()
        raw = gathered[l].astype(F32)
        mean = jnp.sum(jnp.sum(raw, axis=0), axis=0, keepdims=True) / members
        anom[...] = (raw - mean[None]).astype(BF16)
        right = anom[...].reshape(members, half)

        def one_block(b, inner):
            rows_of = pl.ds(pl.multiple_of(b * step, step), step)
            cov = jnp.dot(obs_t[rows_of], right, preferred_element_type=F32)
            gain[rows_of] = (cov * taper[rows_of]).astype(BF16)
            return inner

        lax.fori_loop(0, 3 * kk // step, one_block, 0)
        increment = jnp.dot(
            pert[...].reshape(2 * mm, 3 * kk), gain[...], preferred_element_type=F32
        )
        base = mean[None] + root[None] * anom[pl.ds(2 * q, 2)].astype(F32)
        result[l] = (base + increment.reshape(2, mm, half)).astype(BF16)
        out_local(l).start()
        out_remote(l).start()
        return carry

    lax.fori_loop(0, nl, one_variable, 0)

    def finish(l, carry):
        for j in range(1, nm):
            bulk(l, j).wait_send()
        out_local(l).wait()
        out_remote(l).wait_send()
        out_from(l).wait_recv()
        return carry

    lax.fori_loop(0, nl, finish, 0)
    for i, j in group:
        sum_copy(i, j).wait_send()
    for i in range(1, nd):
        part_copy(i).wait_send()
    for j in range(1, nm):
        square_copy(j, me).wait_send()
        obs_copy(j, me).wait_send()
    for i in range(1, nr):
        total_copy(i, r).wait_send()
    sib_pert(c).wait_send()
    for side in (0, 1):

        @pl.when(has_side[side])
        def _():
            for to in (0, 1):
                side_obs(side, me, 0, to).wait_send()
                for g in range(1, ng):
                    side_obs(side, 2 * ((q + g) % ng) + c, g, to).wait_send()
                side_pert(side, c, to).wait_send()
            stat_copy(side).wait_send()


def solution(mesh):
    nr, nd, nm = (mesh.shape[a] for a in ("region", "depth", "member"))

    def shards(ensemble, obs_weights, obs_tiles, obs_values, obs_error, obs_noise):
        nl, mm, tt = ensemble.shape
        kk = obs_tiles.shape[0]
        ng = nm // 2
        half = tt // 2
        dma = pltpu.SemaphoreType.DMA
        vmem = pl.BlockSpec(memory_space=pltpu.VMEM)
        anywhere = pl.BlockSpec(memory_space=pl.ANY)
        analysis, inflation = pl.pallas_call(
            functools.partial(kernel, (nr, nd, nm, nl, mm, tt, kk)),
            out_shape=(
                jax.ShapeDtypeStruct((nl, mm, tt), BF16),
                jax.ShapeDtypeStruct((1, 1), F32),
            ),
            in_specs=[
                pl.BlockSpec(memory_space=pltpu.SMEM),
                anywhere,
                vmem,
                vmem,
                vmem,
                anywhere,
            ],
            out_specs=(anywhere, vmem),
            scratch_shapes=[
                pltpu.VMEM((nl, mm, tt), BF16),
                pltpu.VMEM((nl, nm, mm, half), BF16),
                pltpu.VMEM((mm, kk), F32),
                pltpu.VMEM((mm, kk), F32),
                pltpu.VMEM((nd, mm, kk), F32),
                pltpu.VMEM((nd * nm, 8, kk), F32),
                pltpu.VMEM((nm, 8, kk), F32),
                pltpu.VMEM((nr, 8, 128), F32),
                pltpu.VMEM((3, 8, kk), F32),
                pltpu.VMEM((nm, mm, 3 * kk), BF16),
                pltpu.VMEM((2, mm, 3 * kk), BF16),
                pltpu.VMEM((3 * kk, nm * mm), BF16),
                pltpu.VMEM((3 * kk, half), F32),
                pltpu.VMEM((nm, mm, half), BF16),
                pltpu.VMEM((3 * kk, half), BF16),
                pltpu.VMEM((nl, 2, mm, half), BF16),
                dma((3,)),
                dma((nl, nm)),
                dma((nl, nm)),
                dma((nd * nm,)),
                dma((nd * nm,)),
                dma((nd,)),
                dma((nd,)),
                dma((nm,)),
                dma((nm,)),
                dma((nm,)),
                dma((nm,)),
                dma((nr,)),
                dma((nr,)),
                dma((2, ng, 2)),
                dma((2, nm)),
                dma((2,)),
                dma((2,)),
                dma((1,)),
                dma((1,)),
                dma((2, 2)),
                dma((2, 2)),
                dma((nl,)),
                dma((nl,)),
                dma((nl,)),
            ],
            compiler_params=pltpu.CompilerParams(
                collective_id=0, has_side_effects=True, vmem_limit_bytes=56 * 1024 * 1024
            ),
        )(
            obs_weights,
            ensemble,
            obs_tiles.reshape(1, kk),
            obs_values.reshape(1, kk),
            obs_error.reshape(1, kk),
            obs_noise,
        )
        return analysis, inflation.reshape(())

    return jax.shard_map(
        shards,
        mesh=mesh,
        in_specs=(
            P("depth", "member", "region"),
            P("depth"),
            P("region"),
            P("region"),
            P("region"),
            P("member", "region"),
        ),
        out_specs=(P("depth", "member", "region"), P()),
        check_vma=False,
    )
```

time: 186 us -> 57.6 us (0.31)
  waiting for transfers between devices: 80.9 us -> 0 us
  Pallas kernels: 0 us -> 52.5 us
  matrix products: 32.7 us -> 0 us
  blocking collectives: 23.2 us -> 0 us
  between operations: 16.5 us -> 2.4 us
  starting transfers between devices: 12.3 us -> 0 us
  other arithmetic: 10.1 us -> 0 us
  local copies, waits for them, and re-layouts: 8.89 us -> 2.56 us
    pallas_call x0 -> x1, Pallas kernels: none -> 52.5 us  [shards(): pl.pallas_call(functools.partial(kernel, (nr, nd, nm, nl, mm, tt, kk)), o...]
    all_gather x2 -> x0, waiting for transfers between devices: 51.5 us -> none  [the longest x1 44.1 us: shards(): lax.all_gather(anomalies, 'member', axis=1, tiled=True)]
    dot_general x9 -> x0, matrix products: 32.7 us -> none  [the longest x8 31.9 us: one_block(): jnp.einsum('ltj,mj->lmt', kalman_gain, perturbed, preferred_element_type=...]
    psum x1 -> x0, waiting for transfers between devices: 25 us -> none  [shards(): predicted = lax.psum(partial_pred, 'depth')]
    psum x2 -> x0, blocking collectives: 23.2 us -> none  [the longest x1 12.3 us: shards(): lax.psum((jnp.sum(innovation * innovation), jnp.sum(obs_spread + obs_erro...]
    ppermute x4 -> x0, starting transfers between devices: 12.2 us -> none  [the longest x2 9.57 us: extended(): before = lax.ppermute(last, axis, up)]
    ppermute x4 -> x0, waiting for transfers between devices: 4.46 us -> none  [the longest x2 2.76 us: extended(): before = lax.ppermute(last, axis, up)]
    convert_element_type x11 -> x0, other arithmetic: 3.16 us -> none  [the longest x1 1.44 us: shards(): (ensemble.astype(jnp.float32) - state_mean[:, None, :]).astype(jnp.bfloat16)]
  transfers between devices with their start and end apart: 7 -> 0, of which waited for: 6 -> 0; matrix products, arithmetic and copies ran while one was open for 1% -> 0% of each run, Pallas kernels for 0% -> 0%
where the time goes in v1:
time: 57.6 us; the launch traced here: 57.4 us
  Pallas kernels  52.5 us (91%)
  local copies, waits for them, and re-layouts  2.56 us (4%)
  between operations  2.4 us (4%)
    pallas_call x1, Pallas kernels, shards(): pl.pallas_call(functools.partial(kernel, (nr, nd, nm, nl, mm, tt, kk)), o...  52.5 us
    unnamed x1, local copies, waits for them, and re-layouts  2.56 us

profile of v1, /device:TPU:0, one launch (start us, length us, event | category | flops | bytes accessed | tf_op | source)
XLA Modules:
  0.0 57.4 jit_solution(7788800081272766576)
XLA Ops:
  0.6 52.5 %shard_map.77 = (bf16[7,96,1024]{2,1,0:T(8,128)(2,1)}, f32[1,1]{1,0:T(1,128)}) custom-call(f32[7]{0:T(128)} %weights.1, bf16[7,96,1024]{2,1,0:T(8,128)(2,1)} %ensemble.1, s32[1,512]{1,0:T(1,128)} %bitcast.4, f32[1,512]{1,0:T(1,128)} %bitcast.5, f32[1,512]{1,0:T(1,128)} %bitcast.6, f32[96,512]{1,0:T(8,128)} %noise.1), custom_call_target="tpu_custom_call" | custom-call | tf_op jit(solution)/shard_map/pallas_call | solution.py:487
  53.1 2.6 %copy.10 = bf16[7,96,1024]{2,1,0:T(8,128)(2,1)} copy(bf16[7,96,1024]{2,1,0:T(8,128)(2,1)} %get-tuple-element.8) | data formatting | bytes 2752512

commit v2 on v1

v2 whole, which is shorter than its diff:
```python
import functools

import jax
import jax.numpy as jnp
from jax import lax
from jax.experimental import pallas as pl
from jax.experimental.pallas import tpu as pltpu
from jax.sharding import PartitionSpec as P

RADIUS = 1024
EARLY = 1
F32 = jnp.float32
BF16 = jnp.bfloat16
MESH = pl.DeviceIdType.MESH


def kernel(
    sizes,
    weights,
    ensemble,
    tiles,
    values,
    errors,
    noise,
    out,
    infl_out,
    own,
    gathered,
    noise_v,
    part,
    part_in,
    squares,
    totals,
    stats,
    obs,
    pert,
    obs_t,
    taper,
    anom,
    means,
    gain,
    result,
    local_sem,
    send_e,
    recv_e,
    send_p,
    recv_p,
    send_q,
    recv_q,
    send_o,
    recv_o,
    send_g,
    recv_g,
    send_z,
    recv_z,
    send_st,
    recv_st,
    send_ps,
    recv_ps,
    send_pz,
    recv_pz,
    send_pf,
    recv_pf,
    send_f,
    recv_f,
    send_out,
    recv_out,
    own_out,
):
    nr, nd, nm, nl, mm, tt, kk = sizes
    ng = nm // 2
    half = tt // 2
    members = nm * mm
    r = lax.axis_index("region")
    d = lax.axis_index("depth")
    me = lax.axis_index("member")
    q = me // 2
    c = me % 2
    sib = 2 * q + (1 - c)
    has_side = (r > 0, r < nr - 1)

    def dev(region=None, depth=None, member=None):
        return {
            "region": r if region is None else region,
            "depth": d if depth is None else depth,
            "member": me if member is None else member,
        }

    def rdma(src, dst, ssem, rsem, device):
        return pltpu.make_async_remote_copy(
            src_ref=src,
            dst_ref=dst,
            send_sem=ssem,
            recv_sem=rsem,
            device_id=device,
            device_id_type=MESH,
        )

    local_own = pltpu.make_async_copy(ensemble, own, local_sem.at[0])
    local_own.start()
    local_half = pltpu.make_async_copy(
        ensemble.at[:, :, pl.ds(pl.multiple_of(c * half, 128), half)],
        gathered.at[:, me],
        local_sem.at[1],
    )
    local_half.start()
    local_noise = pltpu.make_async_copy(noise, noise_v, local_sem.at[2])
    local_noise.start()

    group = [(i, 0) for i in range(1, nd)] + [(0, j) for j in range(1, nm)]
    barrier = pltpu.get_barrier_semaphore()
    signals = 0
    for i, j in group:
        pl.semaphore_signal(
            barrier,
            inc=1,
            device_id=dev(depth=(d + i) % nd, member=(me + j) % nm),
            device_id_type=MESH,
        )
        signals += 1
    for i in range(1, nr):
        pl.semaphore_signal(
            barrier, inc=1, device_id=dev(region=(r + i) % nr), device_id_type=MESH
        )
        signals += 1
    pl.semaphore_wait(barrier, signals)

    def bulk(l, j):
        to = (me + j) % nm
        return rdma(
            ensemble.at[l, :, pl.ds(pl.multiple_of((to % 2) * half, 128), half)],
            gathered.at[l, me],
            send_e.at[l, j],
            recv_e.at[l, me],
            dev(member=to),
        )

    def send_bulk(l):
        for j in range(1, nm):
            bulk(l, j).start()

    send_bulk(0)
    local_own.wait()
    total = own[0].astype(F32) * weights[0]
    for l in range(1, nl):
        total = total + own[l].astype(F32) * weights[l]
    hi = total.astype(BF16)
    rest = total - hi.astype(F32)
    mid = rest.astype(BF16)
    low = (rest - mid.astype(F32)).astype(BF16)
    tile_ids = lax.broadcasted_iota(jnp.int32, (tt, kk), 0)
    onehot = jnp.where(tile_ids == tiles[...], 1.0, 0.0).astype(BF16)
    picked = (
        jnp.dot(hi, onehot, preferred_element_type=F32)
        + jnp.dot(mid, onehot, preferred_element_type=F32)
        + jnp.dot(low, onehot, preferred_element_type=F32)
    )
    part[...] = picked
    def part_copy(i):
        to = (d + i) % nd
        return rdma(part, part_in.at[d], send_p.at[i], recv_p.at[d], dev(depth=to))

    def part_from(i):
        frm = (d + i) % nd
        return rdma(part, part_in.at[frm], send_p.at[i], recv_p.at[frm], dev(depth=frm))

    for i in range(1, nd):
        part_copy(i).start()

    predicted = part[...]
    for i in range(1, nd):
        part_from(i).wait_recv()
        predicted = predicted + part_in[(d + i) % nd]
    own_sum = jnp.sum(predicted, axis=0, keepdims=True)
    spread_in = predicted - own_sum / mm
    own_square = jnp.sum(spread_in * spread_in, axis=0, keepdims=True)
    krow = lax.broadcasted_iota(jnp.int32, (8, kk), 0)
    squares[me] = jnp.where(krow == 0, own_sum, own_square)
    obs[me, :, kk : 2 * kk] = spread_in.astype(BF16)

    def square_copy(j, slot):
        return rdma(
            squares.at[slot],
            squares.at[slot],
            send_q.at[j],
            recv_q.at[slot],
            dev(member=(me + j) % nm),
        )

    def obs_copy(j, slot):
        block = obs.at[slot, :, pl.ds(kk, kk)]
        return rdma(block, block, send_o.at[j], recv_o.at[slot], dev(member=(me + j) % nm))

    def side_obs(side, slot, pair):
        window = 2 * kk if side == 0 else 0
        return rdma(
            obs.at[slot, :, pl.ds(kk, kk)],
            obs.at[slot, :, pl.ds(window, kk)],
            send_z.at[side, pair],
            recv_z.at[1 - side, pair],
            dev(region=r + (2 * side - 1)),
        )

    def obs_forward(w, slot, pair):
        block = obs.at[slot, :, pl.ds(w * kk, kk)]
        return rdma(block, block, send_f.at[w, pair], recv_f.at[w, pair], dev(member=sib))

    def cross(g):
        return 2 * ((q + g) % ng) + c

    def cross_sib(g):
        return 2 * ((q + g) % ng) + (1 - c)

    for j in range(1, nm):
        square_copy(j, me).start()
    for g in range(1, ng):
        obs_copy(2 * g, me).start()
    obs_forward(1, me, 0).start()
    for side in (0, 1):

        @pl.when(has_side[side])
        def _():
            side_obs(side, me, 0).start()

        @pl.when(jnp.logical_not(has_side[side]))
        def _():
            window = 0 if side == 0 else 2 * kk
            obs[:, :, window : window + kk] = jnp.zeros((nm, mm, kk), BF16)
            pert[:, :, window : window + kk] = jnp.zeros((2, mm, kk), BF16)
            stats[2 * side] = jnp.zeros((8, kk), F32)

    def send_rest(l, carry):
        send_bulk(l)
        return carry

    lax.fori_loop(1, nl, send_rest, 0)

    for j in range(1, nm):
        square_copy(j, (me + j) % nm).wait_recv()
    moments = [squares[j] for j in range(nm)]
    obs_mean = sum(m[0:1] for m in moments) / members
    deviation = predicted - obs_mean
    part_in[d] = deviation
    square_sum = sum(
        m[1:2] + mm * (m[0:1] / mm - obs_mean) * (m[0:1] / mm - obs_mean) for m in moments
    )
    spread = square_sum / (members - 1)
    error = errors[...]
    innovation = values[...] - obs_mean
    first = jnp.sum(innovation * innovation, axis=1, keepdims=True)
    second = jnp.sum(spread + error, axis=1, keepdims=True)
    rows = lax.broadcasted_iota(jnp.int32, (8, 128), 0)
    totals[r] = jnp.where(rows == 0, first, second)

    def total_copy(i, slot):
        return rdma(
            totals.at[slot],
            totals.at[slot],
            send_g.at[i],
            recv_g.at[slot],
            dev(region=(r + i) % nr),
        )

    for i in range(1, nr):
        total_copy(i, r).start()

    for g in range(1, ng):
        obs_copy(2 * g, cross(g)).wait_recv()
        for side in (0, 1):

            @pl.when(has_side[side])
            def _():
                side_obs(side, cross(g), g).start()

        obs_forward(1, cross(g), g).start()

    for i in range(1, nr):
        total_copy(i, (r + i) % nr).wait_recv()
    grand = totals[0]
    for i in range(1, nr):
        grand = grand + totals[i]
    inflation = grand[0:1, 0:1] / grand[1:2, 0:1]
    root = jnp.sqrt(inflation)
    infl_out[...] = inflation
    factor = inflation / (inflation * spread + error)
    facts = jnp.where(krow == 0, tiles[...].astype(F32), factor / (members - 1))
    for g in range(nm):
        facts = jnp.where(krow == 2 + g, moments[g][0:1] / mm - obs_mean, facts)
    stats[1] = facts
    local_noise.wait()
    pert[c, :, kk : 2 * kk] = (
        innovation + jnp.sqrt(error) * noise_v[...] - root * part_in[d]
    ).astype(BF16)

    def stat_copy(side):
        return rdma(
            stats.at[1],
            stats.at[2 - 2 * side],
            send_st.at[side],
            recv_st.at[1 - side],
            dev(region=r + (2 * side - 1)),
        )

    def sib_pert(slot):
        block = pert.at[slot, :, pl.ds(kk, kk)]
        return rdma(block, block, send_ps.at[0], recv_ps.at[0], dev(member=sib))

    def side_pert(side):
        window = 2 * kk if side == 0 else 0
        return rdma(
            pert.at[c, :, pl.ds(kk, kk)],
            pert.at[c, :, pl.ds(window, kk)],
            send_pz.at[side],
            recv_pz.at[1 - side],
            dev(region=r + (2 * side - 1)),
        )

    def pert_forward(side, slot):
        block = pert.at[slot, :, pl.ds(2 * kk * side, kk)]
        return rdma(block, block, send_pf.at[side], recv_pf.at[side], dev(member=sib))

    sib_pert(c).start()
    for side in (0, 1):

        @pl.when(has_side[side])
        def _():
            stat_copy(side).start()
            side_pert(side).start()

    lane = (lax.broadcasted_iota(jnp.int32, (kk, half), 1) + c * half).astype(F32)

    def make_taper(w):
        columns = stats[w].T
        position = columns[:, 0:1] + float((w - 1) * tt)
        close = jnp.maximum(0.0, 1.0 - jnp.abs(lane - position) * (1.0 / RADIUS))
        taper[w * kk : (w + 1) * kk] = close * close * columns[:, 1:2]

    def transpose_all(w):
        shifts = stats[w].T
        for g in range(nm):
            block = obs[g, :, w * kk : (w + 1) * kk].astype(F32).T + shifts[:, 2 + g : 3 + g]
            obs_t[w * kk : (w + 1) * kk, g * mm : (g + 1) * mm] = block.astype(BF16)

    step = kk // 2

    def gain_blocks(l, lo, hi):
        right = anom[l].reshape(members, half)

        def one_block(b, inner):
            at = (b + 2 * (b // 2)) if lo == 0 else b
            rows_of = pl.ds(pl.multiple_of(at * step, step), step)
            cov = jnp.dot(obs_t[rows_of], right, preferred_element_type=F32)
            gain[l, rows_of] = (cov * taper[rows_of]).astype(BF16)
            return inner

        lax.fori_loop(lo, hi, one_block, 0)

    def own_window(l, carry):
        for j in range(1, nm):
            slot = (me + j) % nm
            rdma(
                gathered.at[l, slot],
                gathered.at[l, slot],
                send_e.at[l, j],
                recv_e.at[l, slot],
                dev(member=slot),
            ).wait_recv()
        raw = gathered[l].astype(F32)
        mean = jnp.sum(jnp.sum(raw, axis=0), axis=0, keepdims=True) / members
        means[l] = jnp.broadcast_to(mean, (8, half))
        anom[l] = (raw - mean[None]).astype(BF16)
        gain_blocks(l, 2, 4)
        return carry

    make_taper(1)
    for g in range(ng):
        obs_forward(1, cross_sib(g), g).wait_recv()
    transpose_all(1)
    local_half.wait()
    early = min(EARLY, nl)
    own_window(0, 0)

    for g in range(ng):
        for side in (0, 1):

            @pl.when(has_side[side])
            def _():
                side_obs(1 - side, cross(g), g).wait_recv()
                obs_forward(2 * side, cross(g), g).start()

    lax.fori_loop(1, early, own_window, 0)
    for side in (0, 1):

        @pl.when(has_side[side])
        def _():
            rdma(
                stats.at[1],
                stats.at[2 * side],
                send_st.at[side],
                recv_st.at[side],
                dev(region=r + (2 * side - 1)),
            ).wait_recv()

        make_taper(2 * side)

    for side in (0, 1):

        @pl.when(has_side[side])
        def _():
            for g in range(ng):
                obs_forward(2 * side, cross_sib(g), g).wait_recv()

        transpose_all(2 * side)

    for side in (0, 1):

        @pl.when(has_side[side])
        def _():
            side_pert(1 - side).wait_recv()
            pert_forward(side, c).start()


    def out_half(l, which):
        return out.at[l, :, pl.ds(pl.multiple_of(which * half, 128), half)]

    def out_local(l):
        return pltpu.make_async_copy(result.at[l, c], out_half(l, c), own_out.at[l])

    def out_remote(l):
        return rdma(
            result.at[l, 1 - c], out_half(l, c), send_out.at[l], recv_out.at[l], dev(member=sib)
        )

    def out_from(l):
        return rdma(
            result.at[l, 1 - c], out_half(l, 1 - c), send_out.at[l], recv_out.at[l], dev(member=sib)
        )

    def one_variable(l, carry):
        @pl.when(l >= early)
        def _():
            own_window(l, 0)

        gain_blocks(l, 0, 4)

        @pl.when(l == 0)
        def _():
            sib_pert(1 - c).wait_recv()
            for side in (0, 1):

                @pl.when(has_side[side])
                def _():
                    pert_forward(side, 1 - c).wait_recv()

        increment = jnp.dot(
            pert[...].reshape(2 * mm, 3 * kk), gain[l], preferred_element_type=F32
        )
        base = means[l][0:1][None] + root[None] * anom[l, pl.ds(2 * q, 2)].astype(F32)
        result[l] = (base + increment.reshape(2, mm, half)).astype(BF16)
        out_local(l).start()
        out_remote(l).start()
        return carry

    lax.fori_loop(0, nl, one_variable, 0)

    def finish(l, carry):
        for j in range(1, nm):
            bulk(l, j).wait_send()
        out_local(l).wait()
        out_remote(l).wait_send()
        out_from(l).wait_recv()
        return carry

    lax.fori_loop(0, nl, finish, 0)
    for i in range(1, nd):
        part_copy(i).wait_send()
    for j in range(1, nm):
        square_copy(j, me).wait_send()
    for g in range(1, ng):
        obs_copy(2 * g, me).wait_send()
    for g in range(ng):
        obs_forward(1, cross(g), g).wait_send()
    for i in range(1, nr):
        total_copy(i, r).wait_send()
    sib_pert(c).wait_send()
    for side in (0, 1):

        @pl.when(has_side[side])
        def _():
            for g in range(ng):
                side_obs(side, cross(g), g).wait_send()
                obs_forward(2 * side, cross(g), g).wait_send()
            side_pert(side).wait_send()
            pert_forward(side, c).wait_send()
            stat_copy(side).wait_send()


def hand_on(block, out):
    pass


def solution(mesh):
    nr, nd, nm = (mesh.shape[a] for a in ("region", "depth", "member"))

    def shards(ensemble, obs_weights, obs_tiles, obs_values, obs_error, obs_noise):
        nl, mm, tt = ensemble.shape
        kk = obs_tiles.shape[0]
        ng = nm // 2
        half = tt // 2
        dma = pltpu.SemaphoreType.DMA
        vmem = pl.BlockSpec(memory_space=pltpu.VMEM)
        anywhere = pl.BlockSpec(memory_space=pl.ANY)
        analysis, inflation = pl.pallas_call(
            functools.partial(kernel, (nr, nd, nm, nl, mm, tt, kk)),
            out_shape=(
                pltpu.VMEM((nl, mm, tt), BF16),
                jax.ShapeDtypeStruct((1, 1), F32),
            ),
            in_specs=[
                pl.BlockSpec(memory_space=pltpu.SMEM),
                anywhere,
                vmem,
                vmem,
                vmem,
                anywhere,
            ],
            out_specs=(vmem, vmem),
            scratch_shapes=[
                pltpu.VMEM((nl, mm, tt), BF16),
                pltpu.VMEM((nl, nm, mm, half), BF16),
                pltpu.VMEM((mm, kk), F32),
                pltpu.VMEM((mm, kk), F32),
                pltpu.VMEM((nd, mm, kk), F32),
                pltpu.VMEM((nm, 8, kk), F32),
                pltpu.VMEM((nr, 8, 128), F32),
                pltpu.VMEM((3, 8, kk), F32),
                pltpu.VMEM((nm, mm, 3 * kk), BF16),
                pltpu.VMEM((2, mm, 3 * kk), BF16),
                pltpu.VMEM((3 * kk, nm * mm), BF16),
                pltpu.VMEM((3 * kk, half), F32),
                pltpu.VMEM((nl, nm, mm, half), BF16),
                pltpu.VMEM((nl, 8, half), F32),
                pltpu.VMEM((nl, 3 * kk, half), BF16),
                pltpu.VMEM((nl, 2, mm, half), BF16),
                dma((3,)),
                dma((nl, nm)),
                dma((nl, nm)),
                dma((nd,)),
                dma((nd,)),
                dma((nm,)),
                dma((nm,)),
                dma((nm,)),
                dma((nm,)),
                dma((nr,)),
                dma((nr,)),
                dma((2, ng)),
                dma((2, ng)),
                dma((2,)),
                dma((2,)),
                dma((1,)),
                dma((1,)),
                dma((2,)),
                dma((2,)),
                dma((2,)),
                dma((2,)),
                dma((3, ng)),
                dma((3, ng)),
                dma((nl,)),
                dma((nl,)),
                dma((nl,)),
            ],
            compiler_params=pltpu.CompilerParams(
                collective_id=0, has_side_effects=True, vmem_limit_bytes=56 * 1024 * 1024
            ),
        )(
            obs_weights,
            ensemble,
            obs_tiles.reshape(1, kk),
            obs_values.reshape(1, kk),
            obs_error.reshape(1, kk),
            obs_noise,
        )
        analysis = pl.pallas_call(
            hand_on,
            out_shape=jax.ShapeDtypeStruct((nl, mm, tt), BF16),
            in_specs=[anywhere],
            out_specs=anywhere,
            input_output_aliases={0: 0},
        )(analysis)
        return analysis, inflation.reshape(())

    return jax.shard_map(
        shards,
        mesh=mesh,
        in_specs=(
            P("depth", "member", "region"),
            P("depth"),
            P("region"),
            P("region"),
            P("region"),
            P("member", "region"),
        ),
        out_specs=(P("depth", "member", "region"), P()),
        check_vma=False,
    )
```

time: 57.6 us -> 51 us (0.89)
  Pallas kernels: 52.5 us -> 47.4 us
  local copies, waits for them, and re-layouts: 2.56 us -> 1.08 us
    pallas_call x1, Pallas kernels: 52.5 us -> 47.4 us  [shards(): pl.pallas_call(functools.partial(kernel, (nr, nd, nm, nl, mm, tt, kk)), o...]
    unnamed x1, local copies, waits for them, and re-layouts: 2.56 us -> 1.08 us
where the time goes in v2:
time: 51 us; the launch traced here: 50.8 us
  Pallas kernels  47.4 us (93%)
  between operations  2.34 us (5%)
  local copies, waits for them, and re-layouts  1.08 us (2%)
    pallas_call x1, Pallas kernels, shards(): pl.pallas_call(functools.partial(kernel, (nr, nd, nm, nl, mm, tt, kk)), o...  47.4 us
    unnamed x1, local copies, waits for them, and re-layouts  1.08 us

profile of v2, /device:TPU:0, one launch (start us, length us, event | category | flops | bytes accessed | tf_op | source)
XLA Modules:
  0.0 50.8 jit_solution(15821408561598266334)
XLA Ops:
  0.6 47.4 %shard_map.77 = (bf16[7,96,1024]{2,1,0:T(8,128)(2,1)S(1)}, f32[1,1]{1,0:T(1,128)}) custom-call(f32[7]{0:T(128)} %weights.1, bf16[7,96,1024]{2,1,0:T(8,128)(2,1)} %ensemble.1, s32[1,512]{1,0:T(1,128)} %bitcast.4, f32[1,512]{1,0:T(1,128)} %bitcast.5, f32[1,512]{1,0:T(1,128)} %bitcast.6, f32[96,512]{1,0:T(8,128)} %noise.1), custom_call_target="tpu_custom_call" | custom-call | tf_op jit(solution)/shard_map/pallas_call | solution.py:513
  48.0 1.1 %copy.12 = bf16[7,96,1024]{2,1,0:T(8,128)(2,1)} copy(bf16[7,96,1024]{2,1,0:T(8,128)(2,1)S(1)} %shard_map.78) | data formatting | bytes 2752512
  (1 shorter events, 0.0 us)

commit v3 on v2

--- a/solution.py
+++ b/solution.py
@@ -8,7 +8,7 @@
 from jax.sharding import PartitionSpec as P
 
 RADIUS = 1024
-EARLY = 1
+EARLY = 2
 F32 = jnp.float32
 BF16 = jnp.bfloat16
 MESH = pl.DeviceIdType.MESH
@@ -155,7 +155,19 @@
         + jnp.dot(mid, onehot, preferred_element_type=F32)
         + jnp.dot(low, onehot, preferred_element_type=F32)
     )
-    part[...] = picked
+    part_mean = jnp.sum(picked, axis=0, keepdims=True) / mm
+    top = part_mean.astype(BF16).astype(F32)
+    second_row = (part_mean - top).astype(BF16).astype(F32)
+    third_row = part_mean - top - second_row
+    prow = lax.broadcasted_iota(jnp.int32, (16, kk), 0)
+    split = jnp.where(prow == 0, top, jnp.where(prow == 1, second_row, third_row))
+    part[0:mm] = (picked - part_mean).astype(BF16)
+    part[mm : mm + 16] = jnp.where(prow < 3, split, 0.0).astype(BF16)
+
+    def whole(block):
+        values_of = block.astype(F32)
+        return values_of[0:mm] + jnp.sum(values_of[mm : mm + 16], axis=0, keepdims=True)
+
     def part_copy(i):
         to = (d + i) % nd
         return rdma(part, part_in.at[d], send_p.at[i], recv_p.at[d], dev(depth=to))
@@ -167,10 +179,10 @@
     for i in range(1, nd):
         part_copy(i).start()
 
-    predicted = part[...]
+    predicted = whole(part[...])
     for i in range(1, nd):
         part_from(i).wait_recv()
-        predicted = predicted + part_in[(d + i) % nd]
+        predicted = predicted + whole(part_in[(d + i) % nd])
     own_sum = jnp.sum(predicted, axis=0, keepdims=True)
     spread_in = predicted - own_sum / mm
     own_square = jnp.sum(spread_in * spread_in, axis=0, keepdims=True)
@@ -240,7 +252,6 @@
     moments = [squares[j] for j in range(nm)]
     obs_mean = sum(m[0:1] for m in moments) / members
     deviation = predicted - obs_mean
-    part_in[d] = deviation
     square_sum = sum(
         m[1:2] + mm * (m[0:1] / mm - obs_mean) * (m[0:1] / mm - obs_mean) for m in moments
     )
@@ -289,7 +300,7 @@
     stats[1] = facts
     local_noise.wait()
     pert[c, :, kk : 2 * kk] = (
-        innovation + jnp.sqrt(error) * noise_v[...] - root * part_in[d]
+        innovation + jnp.sqrt(error) * noise_v[...] - root * deviation
     ).astype(BF16)
 
     def stat_copy(side):
@@ -388,7 +399,6 @@
                 side_obs(1 - side, cross(g), g).wait_recv()
                 obs_forward(2 * side, cross(g), g).start()
 
-    lax.fori_loop(1, early, own_window, 0)
     for side in (0, 1):
 
         @pl.when(has_side[side])
@@ -412,14 +422,6 @@
 
         transpose_all(2 * side)
 
-    for side in (0, 1):
-
-        @pl.when(has_side[side])
-        def _():
-            side_pert(1 - side).wait_recv()
-            pert_forward(side, c).start()
-
-
     def out_half(l, which):
         return out.at[l, :, pl.ds(pl.multiple_of(which * half, 128), half)]
 
@@ -445,6 +447,15 @@
 
         @pl.when(l == 0)
         def _():
+            for side in (0, 1):
+
+                @pl.when(has_side[side])
+                def _():
+                    side_pert(1 - side).wait_recv()
+                    pert_forward(side, c).start()
+
+            for ahead in range(1, early):
+                own_window(ahead, 0)
             sib_pert(1 - c).wait_recv()
             for side in (0, 1):
 
@@ -529,8 +540,8 @@
                 pltpu.VMEM((nl, mm, tt), BF16),
                 pltpu.VMEM((nl, nm, mm, half), BF16),
                 pltpu.VMEM((mm, kk), F32),
-                pltpu.VMEM((mm, kk), F32),
-                pltpu.VMEM((nd, mm, kk), F32),
+                pltpu.VMEM((mm + 16, kk), BF16),
+                pltpu.VMEM((nd, mm + 16, kk), BF16),
                 pltpu.VMEM((nm, 8, kk), F32),
                 pltpu.VMEM((nr, 8, 128), F32),
                 pltpu.VMEM((3, 8, kk), F32),

time: 51 us -> 49.3 us (0.967)
  Pallas kernels: 47.4 us -> 45.7 us
    pallas_call x1, Pallas kernels: 47.4 us -> 45.7 us  [shards(): pl.pallas_call(functools.partial(kernel, (nr, nd, nm, nl, mm, tt, kk)), o...]
where the time goes in v3:
time: 49.3 us; the launch traced here: 49.1 us
  Pallas kernels  45.7 us (93%)
  between operations  2.34 us (5%)
  local copies, waits for them, and re-layouts  1.08 us (2%)
    pallas_call x1, Pallas kernels, shards(): pl.pallas_call(functools.partial(kernel, (nr, nd, nm, nl, mm, tt, kk)), o...  45.7 us
    unnamed x1, local copies, waits for them, and re-layouts  1.08 us

profile of v3, /device:TPU:0, one launch (start us, length us, event | category | flops | bytes accessed | tf_op | source)
XLA Modules:
  0.0 49.1 jit_solution(3943208805644262984)
XLA Ops:
  0.6 45.7 %shard_map.77 = (bf16[7,96,1024]{2,1,0:T(8,128)(2,1)S(1)}, f32[1,1]{1,0:T(1,128)}) custom-call(f32[7]{0:T(128)} %weights.1, bf16[7,96,1024]{2,1,0:T(8,128)(2,1)} %ensemble.1, s32[1,512]{1,0:T(1,128)} %bitcast.4, f32[1,512]{1,0:T(1,128)} %bitcast.5, f32[1,512]{1,0:T(1,128)} %bitcast.6, f32[96,512]{1,0:T(8,128)} %noise.1), custom_call_target="tpu_custom_call" | custom-call | tf_op jit(solution)/shard_map/pallas_call | solution.py:524
  46.3 1.1 %copy.12 = bf16[7,96,1024]{2,1,0:T(8,128)(2,1)} copy(bf16[7,96,1024]{2,1,0:T(8,128)(2,1)S(1)} %shard_map.78) | data formatting | bytes 2752512
  (1 shorter events, 0.0 us)
